TPU v7x, 128 devices: a whole 4x4x4 slice. The times are simulated.
128 devices in a mesh: layer: 4 (over z_hi, core), dp: 32 (over y, z_lo, x).
Axes of the slice: x: 4, y: 4, z: 4 (z_hi: 2, z_lo: 2; z = z_hi * 2 + z_lo), core: 2. Of those that a mesh axis runs over, the one named last changes fastest.
Arguments:
- out_grads: bfloat16 [4, 128, 16384], P('layer', None, 'dp'), may hold values from -3 to 3
- in_acts: bfloat16 [4, 128, 4096], P('layer', None, 'dp'), may hold values from -3 to 3
- out_basis: bfloat16 [4, 16384, 16384], P('layer', None, 'dp'), may hold values from -0.046875 to 0.046875
- in_basis: bfloat16 [4, 4096, 4096], P('layer', None, 'dp'), may hold values from -0.09375 to 0.09375
- eigenvalues: bfloat16 [4, 16384, 4096], P('layer', 'dp'), may hold values from 0.5 to 50
- out_store: bfloat16 [4, 64, 32, 16384], P('layer', 'dp'), may hold values from -0.046875 to 0.046875
- in_store: bfloat16 [4, 64, 32, 4096], P('layer', 'dp'), may hold values from -0.09375 to 0.09375
- counts: int32 [64], P('dp'), may hold values from 1 to 4096
- winners: int32 [4, 6], replicated, may hold values from 0 to 63
Outputs:
- influence: float32 [4, 6, 32], replicated
All inputs are finite; a program needn't handle non-finite values.
Results may differ from a plain program's by a relative error of at most 0.0055.
Values may be sent and summed in bfloat16 or wider, within the bound.
No kernel may reach another device: no remote copies, remote signals or barrier semaphores. Data moves between devices by JAX's collectives and lax.ppermute only.
A program may use at most 192 MiB of HBM per device.

v0:
```python
import functools
import jax
import jax.numpy as jnp
from jax import lax
from jax.sharding import Mesh
from jax.sharding import PartitionSpec as P

NQ = 4
TQ = 32
WIN = 6
R = 32
SPAN = 128
DP = ("dp_0", "dp_1", "dp_2")
LAYER_DP = ("layer_0", "layer_1", "dp_0", "dp_1", "dp_2")
LAYER = ("layer_0", "layer_1")
damping = 0.1


def in_order(blocks, dim):
    blocks = jnp.moveaxis(blocks, 0, dim)
    shape = blocks.shape
    return blocks.reshape(*shape[:dim], shape[dim] * shape[dim + 1], *shape[dim + 2 :])


def all_blocks(value, axes, turns):
    blocks = value[None]
    for k in turns:
        blocks = lax.all_gather(blocks, axes[k], axis=0, tiled=True)
    block = [lax.axis_size(axes[k]) for k in reversed(turns)]
    blocks = blocks.reshape(*block, *value.shape)
    turned = sorted(range(len(turns)), key=lambda place: turns[len(turns) - 1 - place])
    return blocks.transpose(*turned, *range(len(turns), blocks.ndim)).reshape(-1, *value.shape)


def whole_of(value, axes, turns, dim):
    return in_order(all_blocks(value, axes, turns), dim)


def from_everyone(value, axis):
    count = lax.axis_size(axis)
    return lax.all_to_all(
        jnp.broadcast_to(value[None], (count, *value.shape)), axis, 0, 0, tiled=True
    )


def collect(value, axis, dim):
    return in_order(from_everyone(value, axis), dim)


def over_axes(value, axes):
    return functools.reduce(lax.psum, axes, value)


def on_device(
    out_grads, in_acts, out_basis, in_basis, eigenvalues, out_store, in_store, counts, winners
):
    out_local = out_basis[0]
    in_local = in_basis[0]
    out_width = out_local.shape[1]
    rows = out_local
    turned_out = jnp.dot(
        whole_of(out_grads[0], DP, (1, 0, 2), 1), rows, preferred_element_type=jnp.float32
    ).astype(jnp.bfloat16)
    rows = in_local
    turned_part = jnp.dot(
        collect(in_acts[0], DP, 1), rows, preferred_element_type=jnp.float32
    ).astype(jnp.bfloat16)
    turned_in = collect(turned_part, DP, 1)
    left = turned_out.reshape(NQ, TQ, out_width)
    right = turned_in.reshape(NQ, TQ, turned_in.shape[1])
    product = jnp.einsum("qtf,qtd->qfd", left, right, preferred_element_type=jnp.float32)
    divisor = eigenvalues[0].astype(jnp.float32) + damping
    precond = (product / divisor[None]).astype(jnp.bfloat16)
    alive = (jnp.arange(R, dtype=jnp.int32)[None, :] * SPAN < counts[:, None]).astype(jnp.bfloat16)
    masked = in_store[0] * alive[:, :, None]
    out_slices = lax.all_to_all(out_store[0], DP, split_axis=2, concat_axis=0, tiled=True)
    chosen = winners.reshape(NQ * WIN)
    left_rows = jnp.take(out_slices, chosen, axis=0).reshape(NQ, WIN * R, out_width)
    full_width = turned_in.shape[1]
    in_whole = lax.all_gather(masked, DP, axis=0, tiled=True)
    right_rows = jnp.take(in_whole, chosen, axis=0).reshape(NQ, WIN * R, full_width)
    mapped = jnp.einsum("qfd,qkd->qkf", precond, right_rows, preferred_element_type=jnp.float32)
    partial_value = jnp.sum(mapped * left_rows.astype(jnp.float32), axis=2)
    totals = over_axes(partial_value, LAYER_DP)
    return totals.reshape(NQ, WIN, R)


def solution(mesh):
    torus = Mesh(
        mesh.devices.reshape(2, 2, 4, 2, 4), ("layer_0", "layer_1", "dp_0", "dp_1", "dp_2")
    )
    return jax.shard_map(
        on_device,
        mesh=torus,
        in_specs=(
            P(LAYER, None, DP),
            P(LAYER, None, DP),
            P(LAYER, None, DP),
            P(LAYER, None, DP),
            P(LAYER, DP, None),
            P(LAYER, DP, None, None),
            P(LAYER, DP, None, None),
            P(DP),
            P(),
        ),
        out_specs=P(),
        check_vma=False,
    )
```

profile of v0, /device:TPU:8, one launch (start us, length us, event | category | flops | bytes accessed | tf_op | source)
XLA Modules:
  0.0 420.1 jit_solution(17354535812470855363)
XLA Ops:
  6.5 8.0 %all_gather.13 = bf16[2,128,512]{2,1,0:T(8,128)(2,1)} all-gather(bf16[1,128,512]{2,1,0:T(8,128)(2,1)} %param.9), channel_id=1, replica_groups=mesh['layer_0'=2,'layer_1'=2,'dp_0'=4,'dp_1'=2,'dp_2'=4] {'dp_1'}, dimensions={0}, use_global_device_ids=true | all-gather | bytes 393216 | tf_op jit(solution)/shard_map/all_gather | solution.py:28
  14.6 24.9 %all-gather.6.cloned.1.call-done = bf16[8,128,512]{2,1,0:T(8,128)(2,1)} async-done(((bf16[2,128,512]{2,1,0:T(8,128)(2,1)}), bf16[8,128,512]{2,1,0:T(8,128)(2,1)}) %all-gather.6.cloned.1.call-update) | async-done | bytes 1048592 | tf_op jit(solution)/shard_map/all_gather | solution.py:28
  44.4 8.6 %all-to-all-start = ((bf16[32,128,128]{1,2,0:T(8,128)(2,1)}), bf16[32,128,128]{1,2,0:T(8,128)(2,1)S(1)}, u32[]{:S(2)}, u32[]{:S(2)}) async-start(bf16[32,128,128]{1,2,0:T(8,128)(2,1)} %broadcast_in_dim.46), calls=%async_computation | async-start | bytes 2097152 | tf_op jit(solution)/shard_map/all_to_all | solution.py:41
  53.0 17.2 %copy.22 = bf16[1,2,32,16384]{2,1,3,0:T(2,128)(2,1)} copy(bf16[1,2,32,16384]{3,2,1,0:T(8,128)(2,1)} %param.14) | data formatting | bytes 4194304 | tf_op args[5]
  70.2 8.0 %bitcast_bitcast_fusion = bf16[16384,2,32]{2,1,0:T(2,128)(2,1)} fusion(bf16[1,2,32,16384]{2,1,3,0:T(2,128)(2,1)} %copy.22), kind=kLoop, calls=%fused_computation.22 | loop fusion | bytes 4194304
  78.2 18.2 %reshape.123 = bf16[32,2,16384]{2,1,0:T(2,128)(2,1)} reshape(bf16[16384,2,32]{2,1,0:T(2,128)(2,1)} %bitcast_bitcast_fusion) | data formatting | bytes 4194304
  97.3 8.3 %all-to-all-start.2 = ((bf16[32,2,16384]{2,1,0:T(2,128)(2,1)}), bf16[32,2,16384]{2,1,0:T(2,128)(2,1)S(1)}, u32[]{:S(2)}, u32[]{:S(2)}) async-start(bf16[32,2,16384]{2,1,0:T(2,128)(2,1)} %reshape.123), calls=%async_computation.2 | async-start | bytes 4194304 | tf_op jit(solution)/shard_map/all_to_all | solution.py:76
  107.6 41.9 %all-to-all-done.2 = bf16[32,2,16384]{2,1,0:T(2,128)(2,1)S(1)} async-done(((bf16[32,2,16384]{2,1,0:T(2,128)(2,1)}), bf16[32,2,16384]{2,1,0:T(2,128)(2,1)S(1)}, u32[]{:S(2)}, u32[]{:S(2)}) %all-to-all-start.2) | async-done | bytes 2097184 | tf_op jit(solution)/shard_map/all_to_all | solution.py:76
  150.8 7.3 %all-to-all-start.1 = ((bf16[32,128,128]{2,1,0:T(8,128)(2,1)}), bf16[32,128,128]{2,1,0:T(8,128)(2,1)S(1)}, u32[]{:S(2)}, u32[]{:S(2)}) async-start(bf16[32,128,128]{2,1,0:T(8,128)(2,1)} %broadcast_in_dim.47), calls=%async_computation.1 | async-start | bytes 2097152 | tf_op jit(solution)/shard_map/all_to_all | solution.py:41
  158.1 6.6 %add_bitcast_fusion = f32[512,4096]{1,0:T(8,128)} fusion(bf16[1,512,4096]{2,1,0:T(8,128)(2,1)} %param.13), kind=kLoop, calls=%fused_computation.6 | loop fusion | flops 4194304 | bytes 12582912 | tf_op jit(solution)/shard_map/div | solution.py:73
  164.6 6.6 %reshape.124 = bf16[16384,2,32]{2,1,0:T(2,128)(2,1)} reshape(bf16[32,2,16384]{2,1,0:T(2,128)(2,1)S(1)} %all-to-all-done.2) | data formatting | bytes 4194304
  171.2 17.8 %copy.27 = bf16[2,32,32,512]{3,1,0,2:T(8,128)(2,1)} copy(bf16[2,32,32,512]{1,0,3,2:T(2,128)(2,1)} %bitcast.56) | data formatting | bytes 4194304 | tf_op jit(solution)/shard_map/all_to_all | solution.py:76
  189.0 129.3 %all-to-all-done.1 = bf16[32,128,128]{2,1,0:T(8,128)(2,1)S(1)} async-done(((bf16[32,128,128]{2,1,0:T(8,128)(2,1)}), bf16[32,128,128]{2,1,0:T(8,128)(2,1)S(1)}, u32[]{:S(2)}, u32[]{:S(2)}) %all-to-all-start.1) | async-done | bytes 1048608 | tf_op jit(solution)/shard_map/all_to_all | solution.py:41
  321.9 4.6 %copy.18 = bf16[4,2,4,128,512]{4,3,2,1,0:T(8,128)(2,1)} copy(bf16[4,2,4,128,512]{4,3,1,0,2:T(8,128)(2,1)} %bitcast.60) | data formatting | bytes 8388608 | tf_op jit(solution)/shard_map/transpose | solution.py:32
  326.5 6.4 %copy.19 = bf16[128,32,512]{0,2,1:T(8,128)(2,1)} copy(bf16[128,32,512]{2,0,1:T(8,128)(2,1)} %bitcast.59) | data formatting | bytes 8388608 | tf_op jit(solution)/shard_map/transpose | solution.py:20
  332.9 9.4 %fusion.5 = bf16[128,512]{1,0:T(8,128)(2,1)S(1)} fusion(bf16[128,16384]{0,1:T(8,128)(2,1)} %bitcast.58, bf16[1,16384,512]{2,1,0:T(8,128)(2,1)} %param.11), kind=kOutput, calls=%fused_computation.10 | convolution fusion | flops 2147549184 | bytes 21102592 | tf_op jit(solution)/shard_map/dot_general | solution.py:61
  342.4 10.3 %gather_fusion = bf16[24,32,4096]{2,1,0:T(8,128)(2,1)} fusion(bf16[64,32,4096]{2,1,0:T(8,128)(2,1)} %all-gather.4.cloned.1.call-done, s32[1024]{0:T(1024)S(1)} %pad_clamp_fusion), kind=kCustom, calls=%fused_computation | custom fusion | bytes 12583008 | tf_op jit(solution)/shard_map/jit(_take)/gather | solution.py:81
  352.7 6.1 %bitcast_select_fusion = bf16[4,192,4096]{2,1,0:T(8,128)(2,1)} fusion(pred[4,192]{1,0:T(4,128)(4,1)S(1)} %broadcast_in_dim.42, bf16[4,192,4096]{2,1,0:T(8,128)(2,1)} %bitcast.57), kind=kLoop, calls=%fused_computation.7 | loop fusion | flops 3145728 | bytes 12583680 | tf_op jit(solution)/shard_map/jit(_take)/select_n | solution.py:81
  358.7 14.6 %fusion.4 = f32[4,192]{1,0:T(4,128)S(1)} fusion(bf16[4,192,512]{2,1,0:T(8,128)(2,1)S(1)} %bitcast_select_fusion.1, bf16[4,192,4096]{2,1,0:T(8,128)(2,1)} %bitcast_select_fusion, f32[512,4096]{1,0:T(8,128)} %add_bitcast_fusion, bf16[4,32,512]{2,1,0:T(8,128)(2,1)S(1)} %bitcast.65, bf16[4,32,4096]{2,1,0:T(8,128)(2,1)S(1)} %reshape_reshape.3), kind=kOutput, calls=%fused_computation.9 | convolution fusion | flops 3776052480 | bytes 16649216 | tf_op jit(solution)/shard_map/qfd,qkd->qkf/dot_general | solution.py:82
  373.3 6.4 %psum.35 = f32[4,192]{1,0:T(4,128)S(1)} all-reduce(f32[4,192]{1,0:T(4,128)S(1)} %fusion.4), channel_id=1, replica_groups=mesh['layer_0'=2,'layer_1'=2,'dp_0'=4,'dp_1'=2,'dp_2'=4] {'layer_0'}, use_global_device_ids=true, to_apply=%region_1.2 | all-reduce | flops 768 | bytes 6144 | tf_op jit(solution)/shard_map/psum | solution.py:51
  379.7 2.4 psum.36
  382.2 11.5 %psum.37 = f32[4,192]{1,0:T(4,128)S(1)} all-reduce(f32[4,192]{1,0:T(4,128)S(1)} %psum.36), channel_id=1, replica_groups=mesh['layer_0'=2,'layer_1'=2,'dp_0'=4,'dp_1'=2,'dp_2'=4] {'dp_0'}, use_global_device_ids=true, to_apply=%region_3.4 | all-reduce | flops 768 | bytes 6144 | tf_op jit(solution)/shard_map/psum | solution.py:51
  393.7 4.9 %psum.38 = f32[4,192]{1,0:T(4,128)S(1)} all-reduce(f32[4,192]{1,0:T(4,128)S(1)} %psum.37), channel_id=1, replica_groups=mesh['layer_0'=2,'layer_1'=2,'dp_0'=4,'dp_1'=2,'dp_2'=4] {'dp_1'}, use_global_device_ids=true, to_apply=%region_4.5 | all-reduce | flops 768 | bytes 6144 | tf_op jit(solution)/shard_map/psum | solution.py:51
  398.7 14.3 %psum.39 = f32[4,6,32]{2,1,0:T(8,128)S(1)} all-reduce(f32[4,6,32]{2,1,0:T(8,128)S(1)} %reshape.106), channel_id=1, replica_groups=mesh['layer_0'=2,'layer_1'=2,'dp_0'=4,'dp_1'=2,'dp_2'=4] {'dp_2'}, use_global_device_ids=true, to_apply=%region_5.6 | all-reduce | flops 768 | bytes 6144 | tf_op jit(solution)/shard_map/psum | solution.py:51
  (36 shorter events, 13.3 us)
Async XLA Ops:
  6.5 99.4 %copy-start = (bf16[1,4096,128]{2,1,0:T(8,128)(2,1)S(1)}, bf16[1,4096,128]{2,1,0:T(8,128)(2,1)}, u32[]{:S(2)}) copy-start(bf16[1,4096,128]{2,1,0:T(8,128)(2,1)} %param.12) | copy-start | bytes 3145732
  6.5 33.0 %all-gather.6.cloned.1.call-start = ((), (), s32[]{:S(2)}) async-start(), calls=%async_computation.4 | async-start | bytes 1310720 | tf_op jit(solution)/shard_map/all_gather | solution.py:28
  14.6 307.4 %all-gather.8.cloned.1.call-start = ((), (), s32[]{:S(2)}) async-start(), calls=%async_computation.5 | async-start | bytes 5242880 | tf_op jit(solution)/shard_map/all_gather | solution.py:28
  39.5 302.9 %all-gather.4.cloned.1.call-start = ((), (), s32[]{:S(2)}) async-start(), calls=%async_computation.3 | async-start | bytes 17301504 | tf_op jit(solution)/shard_map/all_gather | solution.py:80
  44.4 52.0 %all-to-all-start = ((bf16[32,128,128]{1,2,0:T(8,128)(2,1)}), bf16[32,128,128]{1,2,0:T(8,128)(2,1)S(1)}, u32[]{:S(2)}, u32[]{:S(2)}) async-start(bf16[32,128,128]{1,2,0:T(8,128)(2,1)} %broadcast_in_dim.46), calls=%async_computation | async-start | bytes 2097152 | tf_op jit(solution)/shard_map/all_to_all | solution.py:41
  78.2 27.4 %copy-start.3 = (s32[4,6]{1,0:T(4,128)S(1)}, s32[4,6]{1,0:T(4,128)}, u32[]{:S(2)}) copy-start(s32[4,6]{1,0:T(4,128)} %param.17) | copy-start | bytes 292
  96.4 1.0 copy-start.2
  97.3 52.2 %all-to-all-start.2 = ((bf16[32,2,16384]{2,1,0:T(2,128)(2,1)}), bf16[32,2,16384]{2,1,0:T(2,128)(2,1)S(1)}, u32[]{:S(2)}, u32[]{:S(2)}) async-start(bf16[32,2,16384]{2,1,0:T(2,128)(2,1)} %reshape.123), calls=%async_computation.2 | async-start | bytes 4194304 | tf_op jit(solution)/shard_map/all_to_all | solution.py:76
  150.8 167.6 %all-to-all-start.1 = ((bf16[32,128,128]{2,1,0:T(8,128)(2,1)}), bf16[32,128,128]{2,1,0:T(8,128)(2,1)S(1)}, u32[]{:S(2)}, u32[]{:S(2)}) async-start(bf16[32,128,128]{2,1,0:T(8,128)(2,1)} %broadcast_in_dim.47), calls=%async_computation.1 | async-start | bytes 2097152 | tf_op jit(solution)/shard_map/all_to_all | solution.py:41
  358.7 54.8 %copy-start.1 = (bf16[1,4096,128]{2,1,0:T(8,128)(2,1)S(1)}, bf16[1,4096,128]{2,1,0:T(8,128)(2,1)}, u32[]{:S(2)}) copy-start(bf16[1,4096,128]{2,1,0:T(8,128)(2,1)} %param.12) | copy-start | bytes 3145732
Sparse Core Ops, SparseCore 0:
  14.7 24.7 all-gather.5
  41.2 58.4 all-gather.7
  101.3 218.5 all-gather.3
where the time goes:
time: 422 us; the launch traced here: 420 us
  waiting for transfers between devices  196 us (46%)
  local copies, waits for them, and re-layouts  97.6 us (23%)
  blocking collectives  47.6 us (11%)
  matrix products  25.7 us (6%)
  starting transfers between devices  24.3 us (6%)
  other arithmetic  15.5 us (4%)
  between operations  13.2 us (3%)
    all_to_all x2, waiting for transfers between devices, from_everyone(): lax.all_to_all(jnp.broadcast_to(value[None], (count, *value.shape)), axis...  129 us
    unnamed x12, local copies, waits for them, and re-layouts  50.9 us
    all_to_all x1, waiting for transfers between devices, on_device(): lax.all_to_all(out_store[0], DP, split_axis=2, concat_axis=0, tiled=True)  41.9 us
    psum x5, blocking collectives, over_axes(): return functools.reduce(lax.psum, axes, value)  39.6 us
    all_gather x2, waiting for transfers between devices, all_blocks(): blocks = lax.all_gather(blocks, axes[k], axis=0, tiled=True)  24.9 us
    all_to_all x1, local copies, waits for them, and re-layouts, on_device(): lax.all_to_all(out_store[0], DP, split_axis=2, concat_axis=0, tiled=True)  17.8 us
    all_to_all x2, starting transfers between devices, from_everyone(): lax.all_to_all(jnp.broadcast_to(value[None], (count, *value.shape)), axis...  15.9 us
    dot_general x1, matrix products, on_device(): jnp.einsum('qfd,qkd->qkf', precond, right_rows, preferred_element_type=jn...  14.6 us
  transfers between devices with their start and end apart: 6, of which 3 were waited for; matrix products, arithmetic and copies ran while one was open for 25% of the time, Pallas kernels for 0%

commit v1 on v0

--- a/solution.py
+++ b/solution.py
@@ -4,6 +4,7 @@
 from jax import lax
 from jax.sharding import Mesh
 from jax.sharding import PartitionSpec as P
+from jax.lax import all_to_all, psum
 
 NQ = 4
 TQ = 32
@@ -14,6 +15,9 @@
 LAYER_DP = ("layer_0", "layer_1", "dp_0", "dp_1", "dp_2")
 LAYER = ("layer_0", "layer_1")
 damping = 0.1
+shape_the_halves = lambda u, mesh_ax: jnp.concatenate(
+    all_to_all(jnp.stack(psum(1, mesh_ax) * [u], axis=0), mesh_ax, 0, 0), axis=0
+)
 
 
 def in_order(blocks, dim):
@@ -25,7 +29,7 @@
 def all_blocks(value, axes, turns):
     blocks = value[None]
     for k in turns:
-        blocks = lax.all_gather(blocks, axes[k], axis=0, tiled=True)
+        blocks = shape_the_halves(blocks, axes[k])
     block = [lax.axis_size(axes[k]) for k in reversed(turns)]
     blocks = blocks.reshape(*block, *value.shape)
     turned = sorted(range(len(turns)), key=lambda place: turns[len(turns) - 1 - place])

time: 422 us -> 456 us (1.081)
  starting transfers between devices: 24.3 us -> 191 us
  waiting for transfers between devices: 196 us -> 36.1 us
  blocking collectives: 47.6 us -> 68.6 us
    all_to_all x2 -> x1, starting transfers between devices: 15.9 us -> 173 us  [from_everyone(): lax.all_to_all(jnp.broadcast_to(value[None], (count, *value.shape)), axis...]
    all_to_all x2 -> x1, waiting for transfers between devices: 129 us -> 0.01 us  [from_everyone(): lax.all_to_all(jnp.broadcast_to(value[None], (count, *value.shape)), axis...]
    all_to_all x0 -> x2, blocking collectives: none -> 30.3 us  [the longest x1 22.1 us: from_everyone(): lax.all_to_all(jnp.broadcast_to(value[None], (count, *value.shape)), axis...]
    all_gather x2 -> x0, waiting for transfers between devices: 24.9 us -> none  [all_blocks(): blocks = lax.all_gather(blocks, axes[k], axis=0, tiled=True)]
    all_to_all x1, waiting for transfers between devices: 41.9 us -> 24.8 us  [on_device(): lax.all_to_all(out_store[0], DP, split_axis=2, concat_axis=0, tiled=True)]
    all_to_all x0 -> x2, waiting for transfers between devices: none -> 11.3 us  [all_to_all(jnp.stack(psum(1, mesh_ax) * [u], axis=0), mesh_ax, 0, 0)]
    all_to_all x0 -> x2, starting transfers between devices: none -> 10.1 us  [all_to_all(jnp.stack(psum(1, mesh_ax) * [u], axis=0), mesh_ax, 0, 0)]
    all_gather x1 -> x0, blocking collectives: 8 us -> none  [all_blocks(): blocks = lax.all_gather(blocks, axes[k], axis=0, tiled=True)]
  transfers between devices with their start and end apart: 6 -> 5, of which waited for: 3 -> 2; matrix products, arithmetic and copies ran while one was open for 25% -> 24% of each run, Pallas kernels for 0% -> 0%
where the time goes in v1:
time: 456 us; the launch traced here: 452 us
  starting transfers between devices  191 us (42%)
  local copies, waits for them, and re-layouts  101 us (22%)
  blocking collectives  68.6 us (15%)
  waiting for transfers between devices  36.1 us (8%)
  matrix products  25.7 us (6%)
  other arithmetic  16.6 us (4%)
  between operations  13.5 us (3%)
    all_to_all x1, starting transfers between devices, from_everyone(): lax.all_to_all(jnp.broadcast_to(value[None], (count, *value.shape)), axis...  173 us
    unnamed x16, local copies, waits for them, and re-layouts  50.9 us
    psum x5, blocking collectives, over_axes(): return functools.reduce(lax.psum, axes, value)  38.3 us
    all_to_all x1, waiting for transfers between devices, on_device(): lax.all_to_all(out_store[0], DP, split_axis=2, concat_axis=0, tiled=True)  24.8 us
    all_to_all x1, blocking collectives, from_everyone(): lax.all_to_all(jnp.broadcast_to(value[None], (count, *value.shape)), axis...  22.1 us
    all_to_all x1, local copies, waits for them, and re-layouts, on_device(): lax.all_to_all(out_store[0], DP, split_axis=2, concat_axis=0, tiled=True)  17.8 us
    dot_general x1, matrix products, on_device(): jnp.einsum('qfd,qkd->qkf', precond, right_rows, preferred_element_type=jn...  14.6 us
    all_to_all x2, waiting for transfers between devices, all_to_all(jnp.stack(psum(1, mesh_ax) * [u], axis=0), mesh_ax, 0, 0)  11.3 us
  transfers between devices with their start and end apart: 5, of which 2 were waited for; matrix products, arithmetic and copies ran while one was open for 24% of the time, Pallas kernels for 0%

profile of v1, /device:TPU:8, one launch (start us, length us, event | category | flops | bytes accessed | tf_op | source)
XLA Modules:
  0.0 452.5 jit_solution(9781915603679080227)
XLA Ops:
  10.3 8.2 %all_to_all.43 = bf16[2,1,128,512]{3,2,1,0:T(8,128)(2,1)S(1)} all-to-all(bf16[2,1,128,512]{3,2,1,0:T(8,128)(2,1)S(1)} %pad_maximum_fusion), channel_id=1, replica_groups=mesh['layer_0'=2,'layer_1'=2,'dp_0'=4,'dp_1'=2,'dp_2'=4] {'dp_1'}, dimensions={0} | all-to-all | bytes 524288 | tf_op jit(solution)/shard_map/all_to_all | solution.py:19
  19.7 5.0 %all-to-all-start.1 = ((bf16[4,2,128,512]{3,2,1,0:T(8,128)(2,1)}), bf16[4,2,128,512]{3,2,1,0:T(8,128)(2,1)S(1)}, u32[]{:S(2)}, u32[]{:S(2)}) async-start(bf16[4,2,128,512]{3,2,1,0:T(8,128)(2,1)} %stack.10), calls=%async_computation.1 | async-start | bytes 2097152 | tf_op jit(solution)/shard_map/all_to_all | solution.py:19
  24.7 17.2 %copy.21 = bf16[1,2,32,16384]{2,1,3,0:T(2,128)(2,1)} copy(bf16[1,2,32,16384]{3,2,1,0:T(8,128)(2,1)} %param.14) | data formatting | bytes 4194304 | tf_op args[5]
  43.3 172.8 %all-to-all-start.3 = ((bf16[32,128,128]{1,2,0:T(8,128)(2,1)}), bf16[32,128,128]{1,2,0:T(8,128)(2,1)S(1)}, u32[]{:S(2)}, u32[]{:S(2)}) async-start(bf16[32,128,128]{1,2,0:T(8,128)(2,1)} %broadcast_in_dim.46), calls=%async_computation.3 | async-start | bytes 2097152 | tf_op jit(solution)/shard_map/all_to_all | solution.py:45
  216.1 8.0 %bitcast_bitcast_fusion = bf16[16384,2,32]{2,1,0:T(2,128)(2,1)} fusion(bf16[1,2,32,16384]{2,1,3,0:T(2,128)(2,1)} %copy.21), kind=kLoop, calls=%fused_computation.23 | loop fusion | bytes 4194304
  224.1 18.2 %reshape.123 = bf16[32,2,16384]{2,1,0:T(2,128)(2,1)} reshape(bf16[16384,2,32]{2,1,0:T(2,128)(2,1)} %bitcast_bitcast_fusion) | data formatting | bytes 4194304
  243.2 8.3 %all-to-all-start.5 = ((bf16[32,2,16384]{2,1,0:T(2,128)(2,1)}), bf16[32,2,16384]{2,1,0:T(2,128)(2,1)S(1)}, u32[]{:S(2)}, u32[]{:S(2)}) async-start(bf16[32,2,16384]{2,1,0:T(2,128)(2,1)} %reshape.123), calls=%async_computation.5 | async-start | bytes 4194304 | tf_op jit(solution)/shard_map/all_to_all | solution.py:80
  253.2 24.8 %all-to-all-done.5 = bf16[32,2,16384]{2,1,0:T(2,128)(2,1)S(1)} async-done(((bf16[32,2,16384]{2,1,0:T(2,128)(2,1)}), bf16[32,2,16384]{2,1,0:T(2,128)(2,1)S(1)}, u32[]{:S(2)}, u32[]{:S(2)}) %all-to-all-start.5) | async-done | bytes 2097184 | tf_op jit(solution)/shard_map/all_to_all | solution.py:80
  278.3 22.1 %all_to_all.44 = bf16[32,128,128]{2,1,0:T(8,128)(2,1)S(1)} all-to-all(bf16[32,128,128]{2,1,0:T(8,128)(2,1)S(1)} %broadcast_in_dim.47), channel_id=1, replica_groups=mesh['layer_0'=2,'layer_1'=2,'dp_0'=4,'dp_1'=2,'dp_2'=4] {'dp_0','dp_1',..., dimensions={0} | all-to-all | bytes 2097152 | tf_op jit(solution)/shard_map/all_to_all | solution.py:45
  304.1 5.0 %all-to-all-start.2 = ((bf16[4,8,128,512]{3,2,1,0:T(8,128)(2,1)}), bf16[4,8,128,512]{3,2,1,0:T(8,128)(2,1)}, u32[]{:S(2)}, u32[]{:S(2)}) async-start(bf16[4,8,128,512]{3,2,1,0:T(8,128)(2,1)} %stack.11), calls=%async_computation.2 | async-start | bytes 8388608 | tf_op jit(solution)/shard_map/all_to_all | solution.py:19
  309.4 6.6 %add_bitcast_fusion = f32[512,4096]{1,0:T(8,128)} fusion(bf16[1,512,4096]{2,1,0:T(8,128)(2,1)} %param.13), kind=kLoop, calls=%fused_computation.6 | loop fusion | flops 4194304 | bytes 12582912 | tf_op jit(solution)/shard_map/div | solution.py:77
  316.0 6.6 %reshape.124 = bf16[16384,2,32]{2,1,0:T(2,128)(2,1)} reshape(bf16[32,2,16384]{2,1,0:T(2,128)(2,1)S(1)} %all-to-all-done.5) | data formatting | bytes 4194304
  322.6 17.8 %copy.26 = bf16[2,32,32,512]{3,1,0,2:T(8,128)(2,1)} copy(bf16[2,32,32,512]{1,0,3,2:T(2,128)(2,1)} %bitcast.60) | data formatting | bytes 4194304 | tf_op jit(solution)/shard_map/all_to_all | solution.py:80
  343.9 11.3 %all-to-all-done.2 = bf16[4,8,128,512]{3,2,1,0:T(8,128)(2,1)} async-done(((bf16[4,8,128,512]{3,2,1,0:T(8,128)(2,1)}), bf16[4,8,128,512]{3,2,1,0:T(8,128)(2,1)}, u32[]{:S(2)}, u32[]{:S(2)}) %all-to-all-start.2) | async-done | bytes 4194336 | tf_op jit(solution)/shard_map/all_to_all | solution.py:19
  355.2 4.6 %copy.17 = bf16[4,8,128,512]{3,2,0,1:T(8,128)(2,1)} copy(bf16[4,8,128,512]{3,2,1,0:T(8,128)(2,1)} %all-to-all-done.2) | data formatting | bytes 8388608 | tf_op jit(solution)/shard_map/all_to_all | solution.py:19
  359.8 6.4 %copy.18 = bf16[128,32,512]{0,2,1:T(8,128)(2,1)} copy(bf16[128,32,512]{2,0,1:T(8,128)(2,1)} %bitcast.63) | data formatting | bytes 8388608 | tf_op jit(solution)/shard_map/transpose | solution.py:24
  366.2 9.4 %fusion.5 = bf16[128,512]{1,0:T(8,128)(2,1)S(1)} fusion(bf16[128,16384]{0,1:T(8,128)(2,1)} %bitcast.62, bf16[1,16384,512]{2,1,0:T(8,128)(2,1)} %param.11), kind=kOutput, calls=%fused_computation.10 | convolution fusion | flops 2147549184 | bytes 21102592 | tf_op jit(solution)/shard_map/dot_general | solution.py:65
  375.7 10.3 %gather_fusion = bf16[24,32,4096]{2,1,0:T(8,128)(2,1)} fusion(bf16[64,32,4096]{2,1,0:T(8,128)(2,1)} %all-gather.2.cloned.1.call-done, s32[1024]{0:T(1024)S(1)} %pad_clamp_fusion), kind=kCustom, calls=%fused_computation | custom fusion | bytes 12583008 | tf_op jit(solution)/shard_map/jit(_take)/gather | solution.py:85
  386.0 6.1 %bitcast_select_fusion = bf16[4,192,4096]{2,1,0:T(8,128)(2,1)} fusion(pred[4,192]{1,0:T(4,128)(4,1)S(1)} %broadcast_in_dim.42, bf16[4,192,4096]{2,1,0:T(8,128)(2,1)} %bitcast.61), kind=kLoop, calls=%fused_computation.7 | loop fusion | flops 3145728 | bytes 12583680 | tf_op jit(solution)/shard_map/jit(_take)/select_n | solution.py:85
  392.0 14.6 %fusion.4 = f32[4,192]{1,0:T(4,128)S(1)} fusion(bf16[4,192,512]{2,1,0:T(8,128)(2,1)S(1)} %bitcast_select_fusion.1, bf16[4,192,4096]{2,1,0:T(8,128)(2,1)} %bitcast_select_fusion, f32[512,4096]{1,0:T(8,128)} %add_bitcast_fusion, bf16[4,32,512]{2,1,0:T(8,128)(2,1)S(1)} %bitcast.70, bf16[4,32,4096]{2,1,0:T(8,128)(2,1)S(1)} %reshape_reshape.7), kind=kOutput, calls=%fused_computation.9 | convolution fusion | flops 3776052480 | bytes 16649216 | tf_op jit(solution)/shard_map/qfd,qkd->qkf/dot_general | solution.py:86
  406.6 6.4 %psum.35 = f32[4,192]{1,0:T(4,128)S(1)} all-reduce(f32[4,192]{1,0:T(4,128)S(1)} %fusion.4), channel_id=1, replica_groups=mesh['layer_0'=2,'layer_1'=2,'dp_0'=4,'dp_1'=2,'dp_2'=4] {'layer_0'}, use_global_device_ids=true, to_apply=%region_1.2 | all-reduce | flops 768 | bytes 6144 | tf_op jit(solution)/shard_map/psum | solution.py:55
  415.5 9.2 %psum.37 = f32[4,192]{1,0:T(4,128)S(1)} all-reduce(f32[4,192]{1,0:T(4,128)S(1)} %psum.36), channel_id=1, replica_groups=mesh['layer_0'=2,'layer_1'=2,'dp_0'=4,'dp_1'=2,'dp_2'=4] {'dp_0'}, use_global_device_ids=true, to_apply=%region_3.4 | all-reduce | flops 768 | bytes 6144 | tf_op jit(solution)/shard_map/psum | solution.py:55
  424.7 4.9 %psum.38 = f32[4,192]{1,0:T(4,128)S(1)} all-reduce(f32[4,192]{1,0:T(4,128)S(1)} %psum.37), channel_id=1, replica_groups=mesh['layer_0'=2,'layer_1'=2,'dp_0'=4,'dp_1'=2,'dp_2'=4] {'dp_1'}, use_global_device_ids=true, to_apply=%region_4.5 | all-reduce | flops 768 | bytes 6144 | tf_op jit(solution)/shard_map/psum | solution.py:55
  429.7 15.3 %psum.39 = f32[4,6,32]{2,1,0:T(8,128)S(1)} all-reduce(f32[4,6,32]{2,1,0:T(8,128)S(1)} %reshape.106), channel_id=1, replica_groups=mesh['layer_0'=2,'layer_1'=2,'dp_0'=4,'dp_1'=2,'dp_2'=4] {'dp_2'}, use_global_device_ids=true, to_apply=%region_5.6 | all-reduce | flops 768 | bytes 6144 | tf_op jit(solution)/shard_map/psum | solution.py:55
  (40 shorter events, 20.0 us)
Async XLA Ops:
  6.5 245.0 %copy-start = (bf16[1,4096,128]{2,1,0:T(8,128)(2,1)S(1)}, bf16[1,4096,128]{2,1,0:T(8,128)(2,1)}, u32[]{:S(2)}) copy-start(bf16[1,4096,128]{2,1,0:T(8,128)(2,1)} %param.12) | copy-start | bytes 3145732
  6.5 369.1 %all-gather.2.cloned.1.call-start = ((), (), s32[]{:S(2)}) async-start(), calls=%async_computation.6 | async-start | bytes 17301504 | tf_op jit(solution)/shard_map/all_gather | solution.py:84
  19.7 22.2 %copy-start.4 = (bf16[1,128,128]{2,1,0:T(8,128)(2,1)S(1)}, bf16[1,128,128]{2,1,0:T(8,128)(2,1)}, u32[]{:S(2)}) copy-start(bf16[1,128,128]{2,1,0:T(8,128)(2,1)} %param.10) | copy-start | bytes 98308
  19.7 22.3 %all-to-all-start.1 = ((bf16[4,2,128,512]{3,2,1,0:T(8,128)(2,1)}), bf16[4,2,128,512]{3,2,1,0:T(8,128)(2,1)S(1)}, u32[]{:S(2)}, u32[]{:S(2)}) async-start(bf16[4,2,128,512]{3,2,1,0:T(8,128)(2,1)} %stack.10), calls=%async_computation.1 | async-start | bytes 2097152 | tf_op jit(solution)/shard_map/all_to_all | solution.py:19
  42.0 182.1 %copy-start.2 = (bf16[4,2,128,512]{3,2,1,0:T(8,128)(2,1)}, bf16[4,2,128,512]{3,2,1,0:T(8,128)(2,1)S(1)}, u32[]{:S(2)}) copy-start(bf16[4,2,128,512]{3,2,1,0:T(8,128)(2,1)S(1)} %all-to-all-done.1) | copy-start | bytes 3145732
  43.3 198.9 %all-to-all-start.3 = ((bf16[32,128,128]{1,2,0:T(8,128)(2,1)}), bf16[32,128,128]{1,2,0:T(8,128)(2,1)S(1)}, u32[]{:S(2)}, u32[]{:S(2)}) async-start(bf16[32,128,128]{1,2,0:T(8,128)(2,1)} %broadcast_in_dim.46), calls=%async_computation.3 | async-start | bytes 2097152 | tf_op jit(solution)/shard_map/all_to_all | solution.py:45
  242.2 1.0 copy-start.3
  243.2 34.8 %all-to-all-start.5 = ((bf16[32,2,16384]{2,1,0:T(2,128)(2,1)}), bf16[32,2,16384]{2,1,0:T(2,128)(2,1)S(1)}, u32[]{:S(2)}, u32[]{:S(2)}) async-start(bf16[32,2,16384]{2,1,0:T(2,128)(2,1)} %reshape.123), calls=%async_computation.5 | async-start | bytes 4194304 | tf_op jit(solution)/shard_map/all_to_all | solution.py:80
  300.4 8.7 %copy-start.5 = (s32[4,6]{1,0:T(4,128)S(1)}, s32[4,6]{1,0:T(4,128)}, u32[]{:S(2)}) copy-start(s32[4,6]{1,0:T(4,128)} %param.17) | copy-start | bytes 292
  304.1 51.2 %all-to-all-start.2 = ((bf16[4,8,128,512]{3,2,1,0:T(8,128)(2,1)}), bf16[4,8,128,512]{3,2,1,0:T(8,128)(2,1)}, u32[]{:S(2)}, u32[]{:S(2)}) async-start(bf16[4,8,128,512]{3,2,1,0:T(8,128)(2,1)} %stack.11), calls=%async_computation.2 | async-start | bytes 8388608 | tf_op jit(solution)/shard_map/all_to_all | solution.py:19
  392.0 53.6 %copy-start.1 = (bf16[1,4096,128]{2,1,0:T(8,128)(2,1)S(1)}, bf16[1,4096,128]{2,1,0:T(8,128)(2,1)}, u32[]{:S(2)}) copy-start(bf16[1,4096,128]{2,1,0:T(8,128)(2,1)} %param.12) | copy-start | bytes 3145732
Sparse Core Ops, SparseCore 0:
  9.4 190.7 all-gather.1
